TPU v7x, 128 devices: a whole 4x4x4 slice. The times are simulated.
128 devices in a mesh: row: 8 (over z, core), col: 16 (over x, y).
Axes of the slice: x: 4, y: 4, z: 4, core: 2. Of those that a mesh axis runs over, the one named last changes fastest.
Arguments:
- edge_code: int32 [128, 4096], P(('row', 'col')), may hold values from 0 to 1572863
- edge_weight: bfloat16 [128, 4096], P(('row', 'col')), may hold values from 1 to 64
- edge_count: int32 [128, 128], P(('row', 'col')), may hold values from 0 to 32, as said below
- tile_blocks: int32 [128, 4, 2], P(('row', 'col')), may hold values from 0 to 127
- hub_blocks: int32 [8, 2, 2], P('row'), may hold values from 0 to 127
- node_degree: float32 [128, 512], P(('row', 'col')), may hold values from 1 to 16
Outputs:
- owned_tiles: float32 [512, 512, 512], P(('row', 'col'))
- hub_tiles: float32 [8192, 512], P(('row', 'col'))
Inputs may be any that keep to these rules, and one draw needn't show every extreme that they name: `edge_count`: at most 32 used slots from one device to another; in every draw some device receives 32 used slots from every device, and the loads of destinations differ widely.
All inputs are finite; a program needn't handle non-finite values.
Results may differ from a plain program's by a relative error of at most 0.0003.
Values may be sent and summed in bfloat16 or wider, within the bound.
A program may use at most 64 MiB of HBM per device.

v0:
```python
import jax
import jax.numpy as jnp
from jax import lax
from jax.experimental import pallas as pl
from jax.experimental.pallas import tpu as pltpu
from jax.sharding import PartitionSpec as P

TILE = 512
TILES_DEV = 4
HUBS = 2
CAP = 32
N_ROW = 8
N_COL = 16
LANES = 128
CHUNK = 256
CHUNKS = TILES_DEV * TILE // CHUNK
FULL = 1 << 22
SPAN = 2
HUB_SPAN = 8
MESH = pl.DeviceIdType.MESH
F32 = jnp.float32
BF16 = jnp.bfloat16
NT = (((1,), (1,)), ((), ()))


def iota(shape, dim):
    return lax.broadcasted_iota(jnp.int32, shape, dim)


def one_hot(keys, rows):
    wide = jnp.broadcast_to(keys.astype(BF16), (rows, keys.shape[1]))
    return wide == iota((rows, keys.shape[1]), 0).astype(BF16)


def weighted(mask, values):
    return jnp.where(mask, jnp.broadcast_to(values.astype(BF16), mask.shape), jnp.zeros((), BF16))


def ones_where(mask):
    return jnp.where(mask, jnp.ones((), BF16), jnp.zeros((), BF16))


def two_rows(x, index):
    return jnp.concatenate([x[2 * index : 2 * index + 1], x[2 * index + 1 : 2 * index + 2]], axis=1)


def arrange(slots_ref, fields, hub_fields, marks):
    turned = slots_ref[...].reshape(N_ROW * N_COL, LANES).T
    code = turned[0:32].astype(jnp.int32)
    crowded = jnp.max(code.astype(F32), axis=(0, 1), keepdims=True)
    code = code & (FULL - 1)
    weight = turned[32:64]
    cell = turned[64:96].astype(jnp.int32)
    hub_weight = turned[96:128]
    hub_fields[0] = (((cell >> 8) & 1) * 64 + (cell >> 9)).astype(F32)
    hub_fields[1] = (cell & 255).astype(F32)
    hub_fields[2] = hub_weight
    used = jnp.where(hub_weight > 0.0, iota((32, LANES), 0) + HUB_SPAN, 0).astype(F32)
    used = jnp.max(used, axis=(0, 1), keepdims=True)

    chunk = jnp.where(weight > 0.0, code >> 17, CHUNKS)
    member = jnp.concatenate([ones_where(chunk == q) for q in range(CHUNKS)], axis=0)
    upto = ones_where(jnp.logical_or(
        iota((LANES, 256), 0) <= iota((LANES, 256), 1), iota((LANES, 256), 1) >= LANES
    ))
    inside = jnp.dot(member, upto, preferred_element_type=F32)
    inside, lines = inside[:, :LANES], inside[:, LANES:]
    before = ones_where(iota((256, 256), 1) < iota((256, 256), 0))
    base = jnp.dot(before, lines.astype(BF16), preferred_element_type=F32)
    rank = base + inside - 1.0
    place = jnp.full((32, LANES), -1.0, F32)
    for q in range(CHUNKS):
        place = jnp.where(chunk == q, rank[32 * q : 32 * q + 32], place)
    place = place.astype(jnp.int32)
    for q in range(CHUNKS):
        marks[pl.ds(q, 1), :] = base[32 * q : 32 * q + 1]
    marks[pl.ds(8, 1), :] = base[255:256] + lines[255:256]
    marks[pl.ds(9, 1), :] = jnp.broadcast_to(used, (1, LANES))
    marks[pl.ds(10, 6), :] = jnp.broadcast_to(crowded, (6, LANES))

    high, low = (place >> 7).astype(F32), (place & 127).astype(F32)
    parts = (
        (code & 255).astype(F32),
        (((code >> 8) & 1) + 2 * (code >> 17)).astype(F32),
        ((code >> 9) & 255).astype(F32),
        weight,
    )
    moved = jnp.zeros((LANES, LANES), F32)
    for p in range(16):
        mask = one_hot(two_rows(high, p), 32)
        left = jnp.concatenate([weighted(mask, two_rows(part, p)) for part in parts], axis=0)
        right = ones_where(one_hot(two_rows(low, p), LANES))
        moved += lax.dot_general(left, right, NT, preferred_element_type=F32)
    flags = moved[32:64].astype(jnp.int32)
    column = moved[0:32] + ((flags & 1) * 256).astype(F32)
    fields[:, pl.ds(32, 8), :] = jnp.zeros((4, 8, LANES), F32)
    fields[0, 0:32] = moved[64:96] + ((flags >> 1) * 256).astype(F32)
    fields[1, 0:32] = column
    fields[2, 0:32] = column - 256.0
    fields[3, 0:32] = moved[96:128]


def exchange_kernel(
    code_hbm, weight_hbm, count_hbm, degree_hbm,
    fields, hub_fields, marks, degrees_a, degrees_b,
    code_ref, weight_ref, count_ref, wide, own_part, message, relay, slots_ref,
    in_sem, row_send, row_recv, col_send, col_recv, turn_send, turn_recv, local_sem,
):
    row = lax.axis_index("row")
    col = lax.axis_index("col")
    row_peers = [lax.rem(row + k, N_ROW) for k in range(1, N_ROW)]
    col_peers = [lax.rem(col + k, N_COL) for k in range(1, N_COL)]

    barrier = pltpu.get_barrier_semaphore()
    for peer in col_peers:
        pl.semaphore_signal(barrier, inc=1, device_id=(row, peer), device_id_type=MESH)
    for peer in row_peers:
        pl.semaphore_signal(barrier, inc=1, device_id=(peer, col), device_id_type=MESH)
    mine_a, mine_b = degrees_a.at[col, row], degrees_b.at[row, col]
    inputs = [
        pltpu.make_async_copy(src, dst, in_sem.at[i])
        for i, (src, dst) in enumerate((
            (count_hbm, count_ref), (weight_hbm, weight_ref), (code_hbm, code_ref),
            (degree_hbm.at[0], mine_a), (degree_hbm.at[1], mine_b),
        ))
    ]
    for copy in inputs:
        copy.start()
    for copy in inputs:
        copy.wait()

    lane = iota((32, LANES), 1)
    line = iota((32, LANES), 0)
    counts = jnp.where(lane // 4 == line, jnp.broadcast_to(count_ref[...], (32, LANES)), 0)
    spread = ones_where(iota((LANES, LANES), 0) % 4 == iota((LANES, LANES), 1) // CAP)
    counts = jnp.dot(counts.astype(BF16), spread, preferred_element_type=F32)
    for g in range(32):
        wide[pl.ds(g, 1), :] = weight_ref[:, pl.ds(g * LANES, LANES)].astype(F32)
    weights = jnp.where((lane % CAP).astype(F32) < counts, wide[...], 0.0)
    codes = code_ref[...]

    slab = jnp.where(weights > 0.0, (codes >> 15) - 32, -1)
    member = jnp.concatenate([ones_where(slab == j) for j in range(N_COL)], axis=0)
    upto = ones_where(jnp.logical_or(
        iota((LANES, 256), 0) <= iota((LANES, 256), 1), iota((LANES, 256), 1) >= LANES
    ))
    inside = jnp.dot(member, upto, preferred_element_type=F32)
    near = jnp.logical_and(
        iota((256, 256), 0) // 4 == iota((256, 256), 1) // 4, iota((256, 256), 1) < iota((256, 256), 0)
    )
    near = ones_where(near)
    rank = jnp.full((32, LANES), -1.0, F32)
    for half in range(2):
        part = inside[256 * half : 256 * half + 256]
        base = jnp.dot(near, part[:, LANES:].astype(BF16), preferred_element_type=F32)
        part = base + part[:, :LANES] - 1.0
        for j in range(8):
            rank = jnp.where(slab == 8 * half + j, part[32 * j : 32 * j + 32], rank)
    crowded = (jnp.max(rank, axis=(0, 1), keepdims=True) >= CAP).astype(F32) * FULL

    slab = slab.astype(F32)
    cell_low = (codes & 255).astype(F32)
    cell_high = ((codes >> 8) & 127).astype(F32)
    packed = []
    for r in range(N_ROW):
        part = jnp.zeros((N_COL, LANES), F32)
        for h in range(2):
            p = 2 * r + h
            mask = one_hot(two_rows(rank, p), CAP)
            none = jnp.zeros((CAP, 256), BF16)
            right = jnp.concatenate([
                weighted(mask, two_rows(cell_low, p)), none,
                weighted(mask, two_rows(cell_high, p)), weighted(mask, two_rows(weights, p)),
            ], axis=0)
            left = ones_where(one_hot(two_rows(slab, p), N_COL))
            part += lax.dot_general(left, right, NT, preferred_element_type=F32)
        packed.append(part)
    packed = jnp.concatenate(packed, axis=0)
    lanes = iota((LANES, LANES), 1)
    packed = jnp.where(lanes < 96, packed * 256.0 + pltpu.roll(packed, 64, axis=1), packed)

    flagged = codes.astype(F32) + crowded
    for u in range(4):
        left = pltpu.roll(flagged, (LANES - CAP * u) % LANES, axis=1)
        right = pltpu.roll(weights, (LANES + CAP - CAP * u) % LANES, axis=1)
        own_part[pl.ds(u, 32, stride=4), :] = jnp.where(lane < CAP, left, right)
    lines = jnp.where(lanes < 64, own_part[...], packed)
    for d in range(N_ROW * N_COL):
        message[d // N_COL, d % N_COL] = lines[d : d + 1]

    pl.semaphore_wait(barrier, N_ROW + N_COL - 2)

    def send(src, dst, send_sem, recv_sem, device):
        pltpu.make_async_remote_copy(
            src_ref=src, dst_ref=dst, send_sem=send_sem, recv_sem=recv_sem,
            device_id=device, device_id_type=MESH,
        ).start()

    for peer in row_peers:
        send(message.at[peer], relay.at[:, row], row_send.at[0], row_recv.at[0], (peer, col))
    for peer in row_peers:
        send(mine_a, mine_a, row_send.at[1], row_recv.at[1], (peer, col))
    for peer in col_peers:
        send(mine_b, mine_b, turn_send.at[0], turn_recv.at[0], (row, peer))
    own = pltpu.make_async_copy(message.at[row], relay.at[:, row], local_sem.at[0])
    own.start()
    own.wait()
    row_others, col_others = pl.ds(0, N_ROW - 1), pl.ds(0, N_COL - 1)

    def settle(ref, sem):
        pltpu.make_async_copy(ref, ref, sem).wait()

    settle(relay.at[:, row_others], row_recv.at[0])
    for peer in col_peers:
        send(relay.at[peer, :, 0], slots_ref.at[col], col_send.at[0], col_recv.at[0], (row, peer))
    own = pltpu.make_async_copy(relay.at[col, :, 0], slots_ref.at[col], local_sem.at[1])
    own.start()
    settle(degrees_a.at[0, row_others], row_recv.at[1])
    for peer in col_peers:
        send(degrees_a.at[col], degrees_a.at[col], col_send.at[1], col_recv.at[1], (row, peer))
    settle(degrees_b.at[0, col_others], turn_recv.at[0])
    for peer in row_peers:
        send(degrees_b.at[row], degrees_b.at[row], turn_send.at[1], turn_recv.at[1], (peer, col))
    own.wait()
    settle(slots_ref.at[col_others], col_recv.at[0])

    arrange(slots_ref, fields, hub_fields, marks)

    settle(relay.at[:, row_others], row_send.at[0])
    settle(degrees_a.at[0, row_others], row_send.at[1])
    settle(degrees_b.at[0, col_others], turn_send.at[0])
    settle(slots_ref.at[col_others], col_send.at[0])
    settle(degrees_a.at[col_others], col_send.at[1])
    settle(degrees_b.at[row_others], turn_send.at[1])
    settle(degrees_a.at[col_others], col_recv.at[1])
    settle(degrees_b.at[row_others], turn_recv.at[1])


def exchange(code, weight, count, degree):
    vmem = pl.BlockSpec(memory_space=pltpu.VMEM)
    hbm = pl.BlockSpec(memory_space=pltpu.HBM)
    pair = pltpu.SemaphoreType.DMA((2,))
    return pl.pallas_call(
        exchange_kernel,
        out_shape=(
            jax.ShapeDtypeStruct((4, 40, LANES), F32),
            jax.ShapeDtypeStruct((3, 32, LANES), F32),
            jax.ShapeDtypeStruct((16, LANES), F32),
            jax.ShapeDtypeStruct((N_COL, N_ROW, 2, LANES), F32),
            jax.ShapeDtypeStruct((N_ROW, N_COL, 2, LANES), F32),
        ),
        in_specs=[hbm] * 4,
        out_specs=(vmem,) * 5,
        scratch_shapes=[
            pltpu.VMEM((32, LANES), jnp.int32),
            pltpu.VMEM((1, N_ROW * N_COL * CAP), BF16),
            pltpu.VMEM((1, LANES), jnp.int32),
            pltpu.VMEM((32, LANES), F32),
            pltpu.VMEM((LANES, LANES), F32),
            pltpu.VMEM((N_ROW, N_COL, 1, LANES), F32),
            pltpu.VMEM((N_COL, N_ROW, 1, LANES), F32),
            pltpu.VMEM((N_COL, N_ROW, LANES), F32),
            pltpu.SemaphoreType.DMA((5,)),
            pair, pair, pair, pair, pair, pair, pair,
        ],
        compiler_params=pltpu.CompilerParams(
            collective_id=0, has_side_effects=True, vmem_limit_bytes=16 << 20
        ),
    )(code, weight, count, degree)


def stored(block):
    return lax.rem(block, N_COL) * N_ROW + block // N_COL


def tile_kernel(
    fields, hub_fields, marks, degrees_a, degrees_b, blocks_hbm, hubs_hbm,
    owned_ref, hub_out, crowded_out, blocks_ref, hubs_ref, crowded_ref, total, hub_total, staged, hub_ref, gathered,
    in_sem, out_sem, flag_sem,
):
    col = lax.axis_index("col")
    inputs = (
        pltpu.make_async_copy(blocks_hbm, blocks_ref, in_sem.at[0]),
        pltpu.make_async_copy(hubs_hbm, hubs_ref, in_sem.at[1]),
    )
    for copy in inputs:
        copy.start()

    def mark(k):
        return jnp.max(marks[pl.ds(k, 1), :]).astype(jnp.int32)

    starts = [mark(q) for q in range(CHUNKS + 1)]
    used = mark(9) // HUB_SPAN
    crowded_ref[0, 0] = (mark(10) >= FULL).astype(jnp.int32)
    flag_copy = pltpu.make_async_copy(crowded_ref, crowded_out, flag_sem)
    flag_copy.start()

    def degrees_of(block):
        return jnp.concatenate([degrees_a[stored(block)], degrees_b[block]], axis=0)

    def out_copy(q):
        return pltpu.make_async_copy(
            staged.at[q], owned_ref.at[q // 2, pl.ds(CHUNK * (q % 2), CHUNK)], out_sem.at[q]
        )

    def product(b, q):
        def line(f):
            return jnp.concatenate(
                [fields[f, pl.ds(2 * b + i, 1), :] for i in range(2 * SPAN)], axis=1
            )

        left = weighted(one_hot(line(0) - 256.0 * q, CHUNK), line(3))
        right = jnp.concatenate(
            [ones_where(one_hot(line(1), 256)), ones_where(one_hot(line(2), 256))], axis=0
        )
        return lax.dot_general(left, right, NT, preferred_element_type=F32)

    firsts = [starts[q] >> 8 for q in range(CHUNKS)]

    def add_rest(q):
        def add_blocks(i, _):
            total[q % 2] += product(firsts[q] + SPAN * i, q)
            return 0

        blocks = ((starts[q + 1] + 255) >> 8) - firsts[q]
        lax.fori_loop(1, (blocks + SPAN - 1) // SPAN, add_blocks, 0)

    total[0] = product(firsts[0], 0)
    add_rest(0)

    scaling = jnp.sum(degrees_a[...], axis=0) + jnp.sum(degrees_b[...], axis=0)
    scaling = jnp.sum(scaling) / (N_ROW * N_COL * TILE)
    for copy in inputs:
        copy.wait()
    gathered[...] = jnp.ones_like(gathered)
    for t in range(TILES_DEV):
        gathered[pl.ds(4 * t, 4), :] = degrees_of(blocks_ref[0, 0, t])
    hub = col // 8
    gathered[pl.ds(24, 4), :] = degrees_of(hubs_ref[0, hub, 0])
    hub_row = gathered[pl.ds(24 + lax.rem(col, 8) // 2, 1), :]
    gathered[pl.ds(16, 8), :] = pltpu.roll(
        jnp.broadcast_to(hub_row, (8, LANES)), 64 * lax.rem(col, 2), axis=1
    )
    degree_rows = (scaling / gathered[...]).T

    def hub_product(b):
        def line(f):
            return jnp.concatenate(
                [hub_fields[f, pl.ds(HUB_SPAN * b + i, 1), :] for i in range(HUB_SPAN)], axis=1
            )

        return lax.dot_general(
            weighted(one_hot(line(0), LANES), line(2)), ones_where(one_hot(line(1), 256)),
            NT, preferred_element_type=F32,
        )

    for q in range(CHUNKS):
        if q + 1 < CHUNKS:
            total[(q + 1) % 2] = product(firsts[q + 1], q + 1)
        else:
            hub_total[...] = hub_product(0)
        tile = q // 2
        degree = 1.0 / degrees_of(blocks_ref[0, 1, tile])
        for j in range(2):
            rows = degree_rows[:, 4 * tile + 2 * (q % 2) + j][:, None]
            for n in range(4):
                values = total[q % 2, pl.ds(LANES * j, LANES), pl.ds(LANES * n, LANES)]
                values = values * rows * degree[n : n + 1]
                staged[q, pl.ds(LANES * j, LANES), pl.ds(LANES * n, LANES)] = jnp.log(
                    jnp.maximum(values, 1.0)
                )
        out_copy(q).start()
        if q + 1 < CHUNKS:
            add_rest(q + 1)

    def add_hub(b, _):
        hub_total[...] += hub_product(b)
        return 0

    lax.fori_loop(1, used, add_hub, 0)
    hub_degree = 1.0 / degrees_of(hubs_ref[0, hub, 1])
    for n in range(4):
        values = hub_total[pl.ds(64 * (n // 2), 64), pl.ds(LANES * (n % 2), LANES)]
        values = values * degree_rows[0:64, 16:17] * hub_degree[n : n + 1]
        hub_ref[:, pl.ds(LANES * n, LANES)] = jnp.log(jnp.maximum(values, 1.0))
    hub_copy = pltpu.make_async_copy(hub_ref, hub_out, out_sem.at[CHUNKS])
    hub_copy.start()
    flag_copy.wait()
    hub_copy.wait()
    for q in range(CHUNKS):
        out_copy(q).wait()


def tiles(arranged, blocks, hubs):
    vmem = pl.BlockSpec(memory_space=pltpu.VMEM)
    hbm = pl.BlockSpec(memory_space=pltpu.HBM)
    return pl.pallas_call(
        tile_kernel,
        out_shape=(
            jax.ShapeDtypeStruct((TILES_DEV, TILE, TILE), F32),
            jax.ShapeDtypeStruct((HUBS * TILE // N_COL, TILE), F32),
            jax.ShapeDtypeStruct((1, 1), jnp.int32),
        ),
        in_specs=[vmem] * 5 + [hbm, hbm],
        out_specs=(hbm, hbm, hbm),
        scratch_shapes=[
            pltpu.SMEM((1, 2, TILES_DEV), jnp.int32),
            pltpu.SMEM((1, HUBS, 2), jnp.int32),
            pltpu.SMEM((1, 1), jnp.int32),
            pltpu.VMEM((2, CHUNK, TILE), F32),
            pltpu.VMEM((LANES, 256), F32),
            pltpu.VMEM((CHUNKS, CHUNK, TILE), F32),
            pltpu.VMEM((HUBS * TILE // N_COL, TILE), F32),
            pltpu.VMEM((LANES, LANES), F32),
            pltpu.SemaphoreType.DMA((2,)),
            pltpu.SemaphoreType.DMA((CHUNKS + 1,)),
            pltpu.SemaphoreType.DMA(()),
        ],
        compiler_params=pltpu.CompilerParams(vmem_limit_bytes=32 << 20),
    )(*arranged, blocks, hubs)


def dense_hub(code, weight, count, hubs, degree):
    def to_owner(x):
        return lax.all_to_all(
            x.reshape(N_ROW * N_COL, -1), ("row", "col"), split_axis=0, concat_axis=0, tiled=True
        )

    codes, weights, counts = to_owner(code), to_owner(weight), to_owner(count)
    usable = jnp.arange(CAP, dtype=jnp.int32)[None, :] < counts
    weights = jnp.where(usable, weights, jnp.zeros((), BF16)).reshape(-1)
    codes = codes.reshape(-1) - TILES_DEV * TILE * TILE

    def step(turn, sums):
        part = lax.dynamic_slice_in_dim(codes, turn * 512, 512)
        value = lax.dynamic_slice_in_dim(weights, turn * 512, 512)
        left = jnp.where(
            (part >> 9)[:, None] == jnp.arange(HUBS * TILE, dtype=jnp.int32)[None, :],
            value[:, None], jnp.zeros((), BF16),
        )
        right = ((part & 511)[:, None] == jnp.arange(TILE, dtype=jnp.int32)[None, :]).astype(BF16)
        return sums + lax.dot_general(
            left, right, (((0,), (0,)), ((), ())), preferred_element_type=F32
        )

    sums = lax.fori_loop(
        0, codes.shape[0] // 512, step, jnp.zeros((HUBS * TILE, TILE), F32)
    )
    sums = sums.reshape(N_COL, HUBS * TILE // N_COL, TILE)
    sums = jnp.sum(lax.all_to_all(sums, "col", 0, 0, tiled=True), axis=0)
    slab_rows = HUBS * TILE // N_COL
    offset = lax.axis_index("col") * slab_rows
    degrees = to_owner(jnp.broadcast_to(degree, (N_ROW * N_COL, TILE)))
    scaling = jnp.mean(degrees)
    pair = lax.dynamic_index_in_dim(hubs[0], offset // TILE, 0, keepdims=False)
    row_degree = lax.dynamic_index_in_dim(degrees, pair[0], 0, keepdims=False)
    row_degree = lax.dynamic_slice_in_dim(row_degree, lax.rem(offset, TILE), slab_rows)
    col_degree = lax.dynamic_index_in_dim(degrees, pair[1], 0, keepdims=False)
    return jnp.log(
        jnp.maximum(scaling * sums / (row_degree[:, None] * col_degree[None, :]), 1.0)
    )


def in_hbm(x):
    return pltpu.with_memory_space_constraint(x, pltpu.HBM)


def shards(edge_code, edge_weight, edge_count, tile_blocks, hub_blocks, node_degree):
    fields, hub_fields, marks, degrees_a, degrees_b = exchange(
        in_hbm(edge_code.reshape(32, LANES)), in_hbm(edge_weight), in_hbm(edge_count),
        in_hbm(node_degree.reshape(2, 2, LANES)),
    )
    degrees_a, degrees_b = (x.reshape(-1, 2, LANES) for x in (degrees_a, degrees_b))
    owned, hub, crowded = tiles(
        (fields, hub_fields, marks, degrees_a, degrees_b),
        in_hbm(tile_blocks.transpose(0, 2, 1)), in_hbm(hub_blocks),
    )
    def dense(_):
        hub = dense_hub(edge_code, edge_weight, edge_count, hub_blocks, node_degree)
        return jnp.zeros_like(crowded), hub

    _, hub = lax.while_loop(lambda state: state[0][0, 0] > 0, dense, (crowded, hub))
    return owned, hub


def solution(mesh):
    both = ("row", "col")
    return jax.shard_map(
        shards,
        mesh=mesh,
        in_specs=(
            P(both, None), P(both, None), P(both, None),
            P(both, None, None), P("row", None, None), P(both, None),
        ),
        out_specs=(P(both, None, None), P(both, None)),
        check_vma=False,
    )
```

profile of v0, /device:TPU:0, one launch (start us, length us, event | category | flops | bytes accessed | tf_op | source)
XLA Modules:
  0.0 23.6 jit_solution(9323438250396372176)
XLA Ops:
  0.6 17.3 %shard_map.77 = (f32[4,40,128]{2,1,0:T(8,128)S(1)}, f32[3,32,128]{2,1,0:T(8,128)S(1)}, f32[16,128]{1,0:T(8,128)S(1)}, f32[16,8,2,128]{3,2,1,0:T(2,128)S(1)}, f32[8,16,2,128]{3,2,1,0:T(2,128)S(1)}) custom-call(s32[32,128]{1,0:T(8,128)} %bitcast.18, bf16[1,4096]{1,0:T(2,128)(2,1)} %weight_hbm.1, s32[1,128]{1,0:T(1,128)} %count_hbm.1, f32[2,2,128]{2,1,0:T(2,128)} %bitcast.20), custom_call_target="tpu_custom_call" | custom-call | tf_op jit(solution)/shard_map/pallas_call | solution.py:243
  17.9 4.8 %shard_map.78 = (f32[4,512,512]{2,1,0:T(8,128)}, f32[64,512]{1,0:T(8,128)}, s32[1,1]{1,0:T(1,128)}) custom-call(f32[4,40,128]{2,1,0:T(8,128)S(1)} %get-tuple-element.124.fields, f32[3,32,128]{2,1,0:T(8,128)S(1)} %get-tuple-element.125.hub_fields, f32[16,128]{1,0:T(8,128)S(1)} %get-tuple-element.126.marks, f32[128,2,128]{2,1,0:T(2,128)S(1)} %bitcast.15, ...), custom_call_target="tpu_custom_call" | custom-call | tf_op jit(solution)/shard_map/pallas_call | solution.py:397
  22.7 0.8 %while.21 = (s32[1,1]{1,0:T(1,128)}, f32[64,512]{1,0:T(8,128)}, f32[1,512]{1,0:T(1,128)}, s32[1,4096]{1,0:T(1,128)}, s32[1,128]{1,0:T(1,128)}, /*index=5*/bf16[1,4096]{1,0:T(2,128)(2,1)}, s32[1,2,2]{2,1,0:T(2,128)}) while((s32[1,1]{1,0:T(1,128)}, f32[64,512]{1,0:T(8,128)}, f32[1,512]{1,0:T(1,128)}, s32[1,4096]{1,0:T(1,128)}, s32[1,128]{1,0:T(1,128)}, ...), condition=%region_5.6_spmd, body=%region_0.5_spmd | while | flops 539931648 | bytes 23348980 | solution.py:482
where the time goes:
time: 23.8 us; the launch traced here: 23.6 us
  Pallas kernels  22 us (92%)
  between operations  0.81 us (3%)
  loops' own time  0.79 us (3%)
    pallas_call x1, Pallas kernels, exchange(): pl.pallas_call(exchange_kernel, out_shape=(jax.ShapeDtypeStruct((4, 40, L...  17.3 us
    pallas_call x1, Pallas kernels, tiles(): pl.pallas_call(tile_kernel, out_shape=(jax.ShapeDtypeStruct((TILES_DEV, T...  4.75 us
    another operation x1, loops' own time, shards(): lax.while_loop(lambda state: state[0][0, 0] > 0, dense, (crowded, hub))  0.79 us

commit v1 on v0

--- a/solution.py
+++ b/solution.py
@@ -15,6 +15,7 @@
 CHUNK = 256
 CHUNKS = TILES_DEV * TILE // CHUNK
 FULL = 1 << 22
+IDS = 11
 SPAN = 2
 HUB_SPAN = 8
 MESH = pl.DeviceIdType.MESH
@@ -76,7 +77,7 @@
         marks[pl.ds(q, 1), :] = base[32 * q : 32 * q + 1]
     marks[pl.ds(8, 1), :] = base[255:256] + lines[255:256]
     marks[pl.ds(9, 1), :] = jnp.broadcast_to(used, (1, LANES))
-    marks[pl.ds(10, 6), :] = jnp.broadcast_to(crowded, (6, LANES))
+    marks[pl.ds(10, 1), :] = jnp.broadcast_to(crowded, (1, LANES))
 
     high, low = (place >> 7).astype(F32), (place & 127).astype(F32)
     parts = (
@@ -101,31 +102,34 @@
 
 
 def exchange_kernel(
-    code_hbm, weight_hbm, count_hbm, degree_hbm,
+    code_hbm, weight_hbm, count_hbm, degree_hbm, blocks_hbm, hubs_hbm,
     fields, hub_fields, marks, degrees_a, degrees_b,
-    code_ref, weight_ref, count_ref, wide, own_part, message, relay, slots_ref,
+    code_ref, weight_ref, count_ref, blocks_ref, hubs_ref, wide, own_part, message, relay, slots_ref,
     in_sem, row_send, row_recv, col_send, col_recv, turn_send, turn_recv, local_sem,
 ):
     row = lax.axis_index("row")
     col = lax.axis_index("col")
-    row_peers = [lax.rem(row + k, N_ROW) for k in range(1, N_ROW)]
-    col_peers = [lax.rem(col + k, N_COL) for k in range(1, N_COL)]
-
-    barrier = pltpu.get_barrier_semaphore()
-    for peer in col_peers:
-        pl.semaphore_signal(barrier, inc=1, device_id=(row, peer), device_id_type=MESH)
-    for peer in row_peers:
-        pl.semaphore_signal(barrier, inc=1, device_id=(peer, col), device_id_type=MESH)
+    row_peers = [lax.rem(row + k, N_ROW) for k in (4, 3, 5, 2, 6, 1, 7)]
+    col_peers = [
+        lax.rem(col + k, N_COL) for k in (10, 6, 9, 11, 5, 7, 8, 2, 14, 13, 3, 12, 4, 1, 15)
+    ]
+
     mine_a, mine_b = degrees_a.at[col, row], degrees_b.at[row, col]
     inputs = [
         pltpu.make_async_copy(src, dst, in_sem.at[i])
         for i, (src, dst) in enumerate((
             (count_hbm, count_ref), (weight_hbm, weight_ref), (code_hbm, code_ref),
             (degree_hbm.at[0], mine_a), (degree_hbm.at[1], mine_b),
+            (blocks_hbm, blocks_ref), (hubs_hbm, hubs_ref),
         ))
     ]
     for copy in inputs:
         copy.start()
+    barrier = pltpu.get_barrier_semaphore()
+    for peer in col_peers:
+        pl.semaphore_signal(barrier, inc=1, device_id=(row, peer), device_id_type=MESH)
+    for peer in row_peers:
+        pl.semaphore_signal(barrier, inc=1, device_id=(peer, col), device_id_type=MESH)
     for copy in inputs:
         copy.wait()
 
@@ -225,6 +229,10 @@
     settle(slots_ref.at[col_others], col_recv.at[0])
 
     arrange(slots_ref, fields, hub_fields, marks)
+    ids = [blocks_ref[0, side, t] for side in range(2) for t in range(TILES_DEV)]
+    ids += [hubs_ref[0, col // 8, side] for side in range(2)]
+    for k, block in enumerate(ids):
+        marks[pl.ds(IDS + k, 1), :] = jnp.full((1, LANES), block, jnp.int32).astype(F32)
 
     settle(relay.at[:, row_others], row_send.at[0])
     settle(degrees_a.at[0, row_others], row_send.at[1])
@@ -236,7 +244,7 @@
     settle(degrees_b.at[row_others], turn_recv.at[1])
 
 
-def exchange(code, weight, count, degree):
+def exchange(code, weight, count, degree, blocks, hubs):
     vmem = pl.BlockSpec(memory_space=pltpu.VMEM)
     hbm = pl.BlockSpec(memory_space=pltpu.HBM)
     pair = pltpu.SemaphoreType.DMA((2,))
@@ -245,28 +253,30 @@
         out_shape=(
             jax.ShapeDtypeStruct((4, 40, LANES), F32),
             jax.ShapeDtypeStruct((3, 32, LANES), F32),
-            jax.ShapeDtypeStruct((16, LANES), F32),
+            jax.ShapeDtypeStruct((24, LANES), F32),
             jax.ShapeDtypeStruct((N_COL, N_ROW, 2, LANES), F32),
             jax.ShapeDtypeStruct((N_ROW, N_COL, 2, LANES), F32),
         ),
-        in_specs=[hbm] * 4,
+        in_specs=[hbm] * 6,
         out_specs=(vmem,) * 5,
         scratch_shapes=[
             pltpu.VMEM((32, LANES), jnp.int32),
             pltpu.VMEM((1, N_ROW * N_COL * CAP), BF16),
             pltpu.VMEM((1, LANES), jnp.int32),
+            pltpu.SMEM((1, 2, TILES_DEV), jnp.int32),
+            pltpu.SMEM((1, HUBS, 2), jnp.int32),
             pltpu.VMEM((32, LANES), F32),
             pltpu.VMEM((LANES, LANES), F32),
             pltpu.VMEM((N_ROW, N_COL, 1, LANES), F32),
             pltpu.VMEM((N_COL, N_ROW, 1, LANES), F32),
             pltpu.VMEM((N_COL, N_ROW, LANES), F32),
-            pltpu.SemaphoreType.DMA((5,)),
+            pltpu.SemaphoreType.DMA((7,)),
             pair, pair, pair, pair, pair, pair, pair,
         ],
         compiler_params=pltpu.CompilerParams(
             collective_id=0, has_side_effects=True, vmem_limit_bytes=16 << 20
         ),
-    )(code, weight, count, degree)
+    )(code, weight, count, degree, blocks, hubs)
 
 
 def stored(block):
@@ -274,17 +284,11 @@
 
 
 def tile_kernel(
-    fields, hub_fields, marks, degrees_a, degrees_b, blocks_hbm, hubs_hbm,
-    owned_ref, hub_out, crowded_out, blocks_ref, hubs_ref, crowded_ref, total, hub_total, staged, hub_ref, gathered,
-    in_sem, out_sem, flag_sem,
+    fields, hub_fields, marks, degrees_a, degrees_b,
+    owned_ref, hub_out, crowded_out, crowded_ref, total, hub_total, staged, hub_ref, gathered,
+    out_sem, flag_sem,
 ):
     col = lax.axis_index("col")
-    inputs = (
-        pltpu.make_async_copy(blocks_hbm, blocks_ref, in_sem.at[0]),
-        pltpu.make_async_copy(hubs_hbm, hubs_ref, in_sem.at[1]),
-    )
-    for copy in inputs:
-        copy.start()
 
     def mark(k):
         return jnp.max(marks[pl.ds(k, 1), :]).astype(jnp.int32)
@@ -295,6 +299,10 @@
     flag_copy = pltpu.make_async_copy(crowded_ref, crowded_out, flag_sem)
     flag_copy.start()
 
+    row_blocks = [mark(IDS + t) for t in range(TILES_DEV)]
+    col_blocks = [mark(IDS + TILES_DEV + t) for t in range(TILES_DEV)]
+    hub_row_block, hub_col_block = mark(IDS + 2 * TILES_DEV), mark(IDS + 2 * TILES_DEV + 1)
+
     def degrees_of(block):
         return jnp.concatenate([degrees_a[stored(block)], degrees_b[block]], axis=0)
 
@@ -330,13 +338,10 @@
 
     scaling = jnp.sum(degrees_a[...], axis=0) + jnp.sum(degrees_b[...], axis=0)
     scaling = jnp.sum(scaling) / (N_ROW * N_COL * TILE)
-    for copy in inputs:
-        copy.wait()
     gathered[...] = jnp.ones_like(gathered)
     for t in range(TILES_DEV):
-        gathered[pl.ds(4 * t, 4), :] = degrees_of(blocks_ref[0, 0, t])
-    hub = col // 8
-    gathered[pl.ds(24, 4), :] = degrees_of(hubs_ref[0, hub, 0])
+        gathered[pl.ds(4 * t, 4), :] = degrees_of(row_blocks[t])
+    gathered[pl.ds(24, 4), :] = degrees_of(hub_row_block)
     hub_row = gathered[pl.ds(24 + lax.rem(col, 8) // 2, 1), :]
     gathered[pl.ds(16, 8), :] = pltpu.roll(
         jnp.broadcast_to(hub_row, (8, LANES)), 64 * lax.rem(col, 2), axis=1
@@ -360,7 +365,7 @@
         else:
             hub_total[...] = hub_product(0)
         tile = q // 2
-        degree = 1.0 / degrees_of(blocks_ref[0, 1, tile])
+        degree = 1.0 / degrees_of(col_blocks[tile])
         for j in range(2):
             rows = degree_rows[:, 4 * tile + 2 * (q % 2) + j][:, None]
             for n in range(4):
@@ -378,7 +383,7 @@
         return 0
 
     lax.fori_loop(1, used, add_hub, 0)
-    hub_degree = 1.0 / degrees_of(hubs_ref[0, hub, 1])
+    hub_degree = 1.0 / degrees_of(hub_col_block)
     for n in range(4):
         values = hub_total[pl.ds(64 * (n // 2), 64), pl.ds(LANES * (n % 2), LANES)]
         values = values * degree_rows[0:64, 16:17] * hub_degree[n : n + 1]
@@ -391,7 +396,7 @@
         out_copy(q).wait()
 
 
-def tiles(arranged, blocks, hubs):
+def tiles(*arranged):
     vmem = pl.BlockSpec(memory_space=pltpu.VMEM)
     hbm = pl.BlockSpec(memory_space=pltpu.HBM)
     return pl.pallas_call(
@@ -401,23 +406,20 @@
             jax.ShapeDtypeStruct((HUBS * TILE // N_COL, TILE), F32),
             jax.ShapeDtypeStruct((1, 1), jnp.int32),
         ),
-        in_specs=[vmem] * 5 + [hbm, hbm],
+        in_specs=[vmem] * 5,
         out_specs=(hbm, hbm, hbm),
         scratch_shapes=[
-            pltpu.SMEM((1, 2, TILES_DEV), jnp.int32),
-            pltpu.SMEM((1, HUBS, 2), jnp.int32),
             pltpu.SMEM((1, 1), jnp.int32),
             pltpu.VMEM((2, CHUNK, TILE), F32),
             pltpu.VMEM((LANES, 256), F32),
             pltpu.VMEM((CHUNKS, CHUNK, TILE), F32),
             pltpu.VMEM((HUBS * TILE // N_COL, TILE), F32),
             pltpu.VMEM((LANES, LANES), F32),
-            pltpu.SemaphoreType.DMA((2,)),
             pltpu.SemaphoreType.DMA((CHUNKS + 1,)),
             pltpu.SemaphoreType.DMA(()),
         ],
         compiler_params=pltpu.CompilerParams(vmem_limit_bytes=32 << 20),
-    )(*arranged, blocks, hubs)
+    )(*arranged)
 
 
 def dense_hub(code, weight, count, hubs, degree):
@@ -468,13 +470,11 @@
 def shards(edge_code, edge_weight, edge_count, tile_blocks, hub_blocks, node_degree):
     fields, hub_fields, marks, degrees_a, degrees_b = exchange(
         in_hbm(edge_code.reshape(32, LANES)), in_hbm(edge_weight), in_hbm(edge_count),
-        in_hbm(node_degree.reshape(2, 2, LANES)),
+        in_hbm(node_degree.reshape(2, 2, LANES)), in_hbm(tile_blocks.transpose(0, 2, 1)),
+        in_hbm(hub_blocks),
     )
     degrees_a, degrees_b = (x.reshape(-1, 2, LANES) for x in (degrees_a, degrees_b))
-    owned, hub, crowded = tiles(
-        (fields, hub_fields, marks, degrees_a, degrees_b),
-        in_hbm(tile_blocks.transpose(0, 2, 1)), in_hbm(hub_blocks),
-    )
+    owned, hub, crowded = tiles(fields, hub_fields, marks, degrees_a, degrees_b)
     def dense(_):
         hub = dense_hub(edge_code, edge_weight, edge_count, hub_blocks, node_degree)
         return jnp.zeros_like(crowded), hub

time: 23.8 us -> 23.2 us (0.975)
  Pallas kernels: 22 us -> 21.4 us
    pallas_call x1, Pallas kernels: 4.75 us -> 4.27 us  [tiles(): pl.pallas_call(tile_kernel, out_shape=(jax.ShapeDtypeStruct((TILES_DEV, T...]
where the time goes in v1:
time: 23.2 us; the launch traced here: 23 us
  Pallas kernels  21.4 us (92%)
  between operations  0.81 us (3%)
  loops' own time  0.79 us (3%)
    pallas_call x1, Pallas kernels, exchange(): pl.pallas_call(exchange_kernel, out_shape=(jax.ShapeDtypeStruct((4, 40, L...  17.1 us
    pallas_call x1, Pallas kernels, tiles(): pl.pallas_call(tile_kernel, out_shape=(jax.ShapeDtypeStruct((TILES_DEV, T...  4.27 us
    another operation x1, loops' own time, shards(): lax.while_loop(lambda state: state[0][0, 0] > 0, dense, (crowded, hub))  0.79 us

profile of v1, /device:TPU:0, one launch (start us, length us, event | category | flops | bytes accessed | tf_op | source)
XLA Modules:
  0.0 23.0 jit_solution(13485081679420997442)
XLA Ops:
  0.6 17.1 %shard_map.77 = (f32[4,40,128]{2,1,0:T(8,128)S(1)}, f32[3,32,128]{2,1,0:T(8,128)S(1)}, f32[24,128]{1,0:T(8,128)S(1)}, f32[16,8,2,128]{3,2,1,0:T(2,128)S(1)}, f32[8,16,2,128]{3,2,1,0:T(2,128)S(1)}) custom-call(s32[32,128]{1,0:T(8,128)} %bitcast.18, bf16[1,4096]{1,0:T(2,128)(2,1)} %weight_hbm.1, s32[1,128]{1,0:T(1,128)} %count_hbm.1, f32[2,2,128]{2,1,0:T(2,128)} %bitcast.20, ...), custom_call_target="tpu_custom_call" | custom-call | tf_op jit(solution)/shard_map/pallas_call | solution.py:251
  17.7 4.3 %shard_map.78 = (f32[4,512,512]{2,1,0:T(8,128)}, f32[64,512]{1,0:T(8,128)}, s32[1,1]{1,0:T(1,128)}) custom-call(f32[4,40,128]{2,1,0:T(8,128)S(1)} %get-tuple-element.124.fields, f32[3,32,128]{2,1,0:T(8,128)S(1)} %get-tuple-element.125.hub_fields, f32[24,128]{1,0:T(8,128)S(1)} %get-tuple-element.126.marks, f32[128,2,128]{2,1,0:T(2,128)S(1)} %bitcast.15, ...), custom_call_target="tpu_custom_call" | custom-call | tf_op jit(solution)/shard_map/pallas_call | solution.py:402
  22.0 0.8 %while.21 = (s32[1,1]{1,0:T(1,128)}, f32[64,512]{1,0:T(8,128)}, f32[1,512]{1,0:T(1,128)}, s32[1,4096]{1,0:T(1,128)}, s32[1,128]{1,0:T(1,128)}, /*index=5*/bf16[1,4096]{1,0:T(2,128)(2,1)}, s32[1,2,2]{2,1,0:T(2,128)}) while((s32[1,1]{1,0:T(1,128)}, f32[64,512]{1,0:T(8,128)}, f32[1,512]{1,0:T(1,128)}, s32[1,4096]{1,0:T(1,128)}, s32[1,128]{1,0:T(1,128)}, ...), condition=%region_5.6_spmd, body=%region_0.5_spmd | while | flops 539931648 | bytes 23348980 | solution.py:482

commit v2 on v1

--- a/solution.py
+++ b/solution.py
@@ -293,7 +293,7 @@
     def mark(k):
         return jnp.max(marks[pl.ds(k, 1), :]).astype(jnp.int32)
 
-    starts = [mark(q) for q in range(CHUNKS + 1)]
+    starts = [0] + [mark(q) for q in range(1, CHUNKS + 1)]
     used = mark(9) // HUB_SPAN
     crowded_ref[0, 0] = (mark(10) >= FULL).astype(jnp.int32)
     flag_copy = pltpu.make_async_copy(crowded_ref, crowded_out, flag_sem)
@@ -333,8 +333,16 @@
         blocks = ((starts[q + 1] + 255) >> 8) - firsts[q]
         lax.fori_loop(1, (blocks + SPAN - 1) // SPAN, add_blocks, 0)
 
-    total[0] = product(firsts[0], 0)
-    add_rest(0)
+    def hub_product(b):
+        def line(f):
+            return jnp.concatenate(
+                [hub_fields[f, pl.ds(HUB_SPAN * b + i, 1), :] for i in range(HUB_SPAN)], axis=1
+            )
+
+        return lax.dot_general(
+            weighted(one_hot(line(0), LANES), line(2)), ones_where(one_hot(line(1), 256)),
+            NT, preferred_element_type=F32,
+        )
 
     scaling = jnp.sum(degrees_a[...], axis=0) + jnp.sum(degrees_b[...], axis=0)
     scaling = jnp.sum(scaling) / (N_ROW * N_COL * TILE)
@@ -348,22 +356,26 @@
     )
     degree_rows = (scaling / gathered[...]).T
 
-    def hub_product(b):
-        def line(f):
-            return jnp.concatenate(
-                [hub_fields[f, pl.ds(HUB_SPAN * b + i, 1), :] for i in range(HUB_SPAN)], axis=1
-            )
-
-        return lax.dot_general(
-            weighted(one_hot(line(0), LANES), line(2)), ones_where(one_hot(line(1), 256)),
-            NT, preferred_element_type=F32,
-        )
+    total[0] = product(0, 0)
+    hub_total[...] = hub_product(0)
+    add_rest(0)
+
+    def add_hub(b, _):
+        hub_total[...] += hub_product(b)
+        return 0
+
+    lax.fori_loop(1, used, add_hub, 0)
+    hub_degree = 1.0 / degrees_of(hub_col_block)
+    for n in range(4):
+        values = hub_total[pl.ds(64 * (n // 2), 64), pl.ds(LANES * (n % 2), LANES)]
+        values = values * degree_rows[0:64, 16:17] * hub_degree[n : n + 1]
+        hub_ref[:, pl.ds(LANES * n, LANES)] = jnp.log(jnp.maximum(values, 1.0))
+    hub_copy = pltpu.make_async_copy(hub_ref, hub_out, out_sem.at[CHUNKS])
+    hub_copy.start()
 
     for q in range(CHUNKS):
         if q + 1 < CHUNKS:
             total[(q + 1) % 2] = product(firsts[q + 1], q + 1)
-        else:
-            hub_total[...] = hub_product(0)
         tile = q // 2
         degree = 1.0 / degrees_of(col_blocks[tile])
         for j in range(2):
@@ -378,18 +390,6 @@
         if q + 1 < CHUNKS:
             add_rest(q + 1)
 
-    def add_hub(b, _):
-        hub_total[...] += hub_product(b)
-        return 0
-
-    lax.fori_loop(1, used, add_hub, 0)
-    hub_degree = 1.0 / degrees_of(hub_col_block)
-    for n in range(4):
-        values = hub_total[pl.ds(64 * (n // 2), 64), pl.ds(LANES * (n % 2), LANES)]
-        values = values * degree_rows[0:64, 16:17] * hub_degree[n : n + 1]
-        hub_ref[:, pl.ds(LANES * n, LANES)] = jnp.log(jnp.maximum(values, 1.0))
-    hub_copy = pltpu.make_async_copy(hub_ref, hub_out, out_sem.at[CHUNKS])
-    hub_copy.start()
     flag_copy.wait()
     hub_copy.wait()
     for q in range(CHUNKS):

time: 23.2 us -> 22.9 us (0.987)
  Pallas kernels: 21.4 us -> 21.1 us
    pallas_call x1, Pallas kernels: 4.27 us -> 3.97 us  [tiles(): pl.pallas_call(tile_kernel, out_shape=(jax.ShapeDtypeStruct((TILES_DEV, T...]
where the time goes in v2:
time: 22.9 us; the launch traced here: 22.7 us
  Pallas kernels  21.1 us (92%)
  between operations  0.81 us (4%)
  loops' own time  0.79 us (3%)
    pallas_call x1, Pallas kernels, exchange(): pl.pallas_call(exchange_kernel, out_shape=(jax.ShapeDtypeStruct((4, 40, L...  17.1 us
    pallas_call x1, Pallas kernels, tiles(): pl.pallas_call(tile_kernel, out_shape=(jax.ShapeDtypeStruct((TILES_DEV, T...  3.97 us
    another operation x1, loops' own time, shards(): lax.while_loop(lambda state: state[0][0, 0] > 0, dense, (crowded, hub))  0.79 us

profile of v2, /device:TPU:0, one launch (start us, length us, event | category | flops | bytes accessed | tf_op | source)
XLA Modules:
  0.0 22.7 jit_solution(7934762266797257204)
XLA Ops:
  0.6 17.1 %shard_map.77 = (f32[4,40,128]{2,1,0:T(8,128)S(1)}, f32[3,32,128]{2,1,0:T(8,128)S(1)}, f32[24,128]{1,0:T(8,128)S(1)}, f32[16,8,2,128]{3,2,1,0:T(2,128)S(1)}, f32[8,16,2,128]{3,2,1,0:T(2,128)S(1)}) custom-call(s32[32,128]{1,0:T(8,128)} %bitcast.18, bf16[1,4096]{1,0:T(2,128)(2,1)} %weight_hbm.1, s32[1,128]{1,0:T(1,128)} %count_hbm.1, f32[2,2,128]{2,1,0:T(2,128)} %bitcast.20, ...), custom_call_target="tpu_custom_call" | custom-call | tf_op jit(solution)/shard_map/pallas_call | solution.py:251
  17.7 4.0 %shard_map.78 = (f32[4,512,512]{2,1,0:T(8,128)}, f32[64,512]{1,0:T(8,128)}, s32[1,1]{1,0:T(1,128)}) custom-call(f32[4,40,128]{2,1,0:T(8,128)S(1)} %get-tuple-element.124.fields, f32[3,32,128]{2,1,0:T(8,128)S(1)} %get-tuple-element.125.hub_fields, f32[24,128]{1,0:T(8,128)S(1)} %get-tuple-element.126.marks, f32[128,2,128]{2,1,0:T(2,128)S(1)} %bitcast.15, ...), custom_call_target="tpu_custom_call" | custom-call | tf_op jit(solution)/shard_map/pallas_call | solution.py:402
  21.7 0.8 %while.21 = (s32[1,1]{1,0:T(1,128)}, f32[64,512]{1,0:T(8,128)}, f32[1,512]{1,0:T(1,128)}, s32[1,4096]{1,0:T(1,128)}, s32[1,128]{1,0:T(1,128)}, /*index=5*/bf16[1,4096]{1,0:T(2,128)(2,1)}, s32[1,2,2]{2,1,0:T(2,128)}) while((s32[1,1]{1,0:T(1,128)}, f32[64,512]{1,0:T(8,128)}, f32[1,512]{1,0:T(1,128)}, s32[1,4096]{1,0:T(1,128)}, s32[1,128]{1,0:T(1,128)}, ...), condition=%region_5.6_spmd, body=%region_0.5_spmd | while | flops 539931648 | bytes 23348980 | solution.py:482
